TPU v7x, 32 devices: a whole 2x2x4 slice. The times are simulated.
32 devices in a mesh: rep: 2 (over core), ep: 16 (over z, y, x).
Axes of the slice: x: 2, y: 2, z: 4, core: 2. Of those that a mesh axis runs over, the one named last changes fastest.
Arguments:
- tokens: bfloat16 [4096, 2048], P(('rep', 'ep')), may hold values from -6 to 6
- gates: float32 [4096], P(('rep', 'ep')), may hold values from 0.25 to 1
- expert_ids: int32 [4096, 1], P(('rep', 'ep')), may hold values from 0 to 3; in each aligned block of 128 rows (0 to 127, 128 to 255, ...) at most 40 rows name the same one
- weight_in: bfloat16 [2048, 16384], P(None, 'ep'), may hold values from -0.125 to 0.125
- weight_out: bfloat16 [16384, 2048], P('ep'), may hold values from -0.09375 to 0.09375
Outputs:
- mixed: bfloat16 [4096, 2048], P(('rep', 'ep'))
Inputs may be any that keep to these rules, and one draw needn't show every extreme that they name: `expert_ids`: among the 128 rows of one device no expert is named by more than 40 rows, and some expert is named by exactly that many in some devices' rows; every expert is named somewhere.
All inputs are finite; a program needn't handle non-finite values.
Results may differ from a plain program's by a relative error of at most 0.0057.
Values may be sent and summed in bfloat16 or wider, within the bound.
A program may use at most 64 MiB of HBM per device.

v0:
```python
import jax
import jax.numpy as jnp
from jax import lax
from jax.sharding import PartitionSpec as P

SLICES = 4


def from_partner(block, axis, distance):
    count = lax.axis_size(axis)
    route = []
    for low in range(count):
        high = low | 1 << distance
        if high != low and high < count:
            route += [(low, high), (high, low)]
    return lax.ppermute(block, axis, route)


def feed(rows, weight_in, weight_out):
    shape = rows.shape
    flat = rows.reshape(-1, shape[-1])
    hidden = jnp.maximum(jnp.dot(flat, weight_in, preferred_element_type=jnp.float32), 0.0).astype(
        jnp.bfloat16
    )
    result = jnp.dot(hidden, weight_out, preferred_element_type=jnp.float32).astype(jnp.bfloat16)
    return result.reshape(shape[:-1] + (weight_out.shape[1],))


def body(tokens, gates, expert_ids, weight_in, weight_out):
    owner_count = lax.axis_size("ep")
    experts = owner_count // SLICES
    tok_rows = tokens.shape[0]
    width = tokens.shape[1]
    capacity = 3 * tok_rows // (4 * experts)
    spare = tok_rows // (2 * experts)
    expert_of = expert_ids[:, 0]
    same = expert_of[:, None] == expert_of[None, :]
    before = lax.broadcasted_iota(jnp.int32, (tok_rows, tok_rows), 1) < lax.broadcasted_iota(
        jnp.int32, (tok_rows, tok_rows), 0
    )
    place_rank = jnp.sum((same & before).astype(jnp.int32), axis=1)
    spilled = place_rank >= capacity
    seat_pos = jnp.where(spilled, place_rank - capacity, place_rank)
    main_slot = jnp.where(spilled, experts * capacity, expert_of * capacity + seat_pos)
    extra_slot = jnp.where(spilled, expert_of * spare + seat_pos, experts * spare)
    main_buffer = (
        jnp.zeros((experts * capacity + 1, width), jnp.bfloat16).at[main_slot].set(tokens)[:-1]
    )
    extra_buffer = (
        jnp.zeros((experts * spare + 1, width), jnp.bfloat16).at[extra_slot].set(tokens)[:-1]
    )
    quarter = width // SLICES
    lane = lax.axis_index("ep") % SLICES
    low_bit = lane % 2
    high_bit = lane // 2

    def narrow(buffer, seats):
        return (
            buffer.reshape(experts, seats, SLICES, quarter)
            .transpose(0, 2, 1, 3)
            .reshape(owner_count, seats, quarter)
        )

    def widen(rows, seats):
        return (
            rows.reshape(experts, SLICES, seats, quarter)
            .transpose(0, 2, 1, 3)
            .reshape(experts * seats, width)
        )

    def gather_group(rows):
        other = from_partner(rows, "ep", 0)
        pair = jnp.where(low_bit == 0, jnp.stack([rows, other], -2), jnp.stack([other, rows], -2))
        across = from_partner(pair, "ep", 1)
        whole = jnp.where(
            high_bit == 0, jnp.stack([pair, across], -3), jnp.stack([across, pair], -3)
        )
        return whole.reshape(rows.shape[:-1] + (width,))

    def reduce_group(part):
        split = part.reshape(part.shape[:-1] + (2, 2, quarter))
        keep = lax.dynamic_index_in_dim(split, high_bit, 2, keepdims=False)
        sending = lax.dynamic_index_in_dim(split, 1 - high_bit, 2, keepdims=False)
        landed = from_partner(sending, "ep", 1)
        both = jnp.stack([keep, landed], 0)
        mine = lax.dynamic_index_in_dim(both, low_bit, 3, keepdims=False)
        giving = lax.dynamic_index_in_dim(both, 1 - low_bit, 3, keepdims=False)
        taken = from_partner(giving, "ep", 0)
        return jnp.sum(mine.astype(jnp.float32), axis=0) + jnp.sum(
            taken.astype(jnp.float32), axis=0
        )

    summed = reduce_group(
        feed(
            gather_group(
                lax.all_to_all(
                    narrow(main_buffer, capacity), "ep", split_axis=0, concat_axis=0, tiled=True
                )
            ),
            weight_in,
            weight_out,
        )
    )
    own_rows = lax.all_to_all(summed, "ep", split_axis=0, concat_axis=0, tiled=True)
    moved_rows = from_partner(narrow(extra_buffer, spare), "rep", 0)
    summed = reduce_group(
        feed(
            gather_group(lax.all_to_all(moved_rows, "ep", split_axis=0, concat_axis=0, tiled=True)),
            weight_in,
            weight_out,
        )
    )
    far_rows = lax.all_to_all(
        summed.astype(jnp.bfloat16), "ep", split_axis=0, concat_axis=0, tiled=True
    ).astype(summed.dtype)
    far_sums = from_partner(far_rows.astype(jnp.bfloat16), "rep", 0).astype(far_rows.dtype)
    combined = jnp.concatenate([widen(own_rows, capacity), widen(far_sums, spare)], axis=0)
    row_index = jnp.where(
        spilled, experts * capacity + expert_of * spare + seat_pos, expert_of * capacity + seat_pos
    )
    expert_out = combined[row_index]
    return (gates[:, None] * expert_out).astype(jnp.bfloat16)


def solution(mesh):
    in_specs = (
        P(("rep", "ep"), None),
        P(("rep", "ep")),
        P(("rep", "ep"), None),
        P(None, "ep"),
        P("ep", None),
    )
    out_specs = P(("rep", "ep"), None)
    return jax.shard_map(body, mesh=mesh, in_specs=in_specs, out_specs=out_specs, check_vma=False)
```

profile of v0, /device:TPU:0, one launch (start us, length us, event | category | flops | bytes accessed | tf_op | source)
XLA Modules:
  0.0 149.7 jit_solution(4015990323748989319)
XLA Ops:
  0.0 0.9 convert_reduce_fusion.4
  0.9 0.7 fusion.15
  1.6 1.9 %scatter_custom_fusion.1 = bf16[65,2048]{1,0:T(8,128)(2,1)S(1)} fusion(s32[128]{0:T(128)S(1)} %get-tuple-element.10, bf16[128,2048]{1,0:T(8,128)(2,1)} %param.5, bf16[]{:T(256)} %constant.81.clone.1), kind=kCustom, calls=%fused_computation.43 | custom fusion | bytes 266752 | tf_op jit(solution)/shard_map/scatter | solution.py:50
  3.5 0.2 reshape.182
  3.8 0.6 collective-permute-start.4
  4.3 1.3 collective-permute-done.4
  5.6 8.2 %all-to-all-start.2 = ((bf16[16,16,512]{2,1,0:T(8,128)(2,1)}), bf16[16,16,512]{2,1,0:T(8,128)(2,1)S(1)}, u32[]{:S(2)}, u32[]{:S(2)}) async-start(bf16[16,16,512]{2,1,0:T(8,128)(2,1)} %collective-permute-done.4), calls=%async_computation.2 | async-start | bytes 524288 | tf_op jit(solution)/shard_map/all_to_all | solution.py:108
  13.8 2.0 %scatter_custom_fusion = bf16[97,2048]{1,0:T(8,128)(2,1)S(1)} fusion(s32[128]{0:T(128)S(1)} %get-tuple-element.11, bf16[128,2048]{1,0:T(8,128)(2,1)} %param.5, bf16[]{:T(256)} %constant.81.clone.1), kind=kCustom, calls=%fused_computation.41 | custom fusion | bytes 397824 | tf_op jit(solution)/shard_map/scatter | solution.py:47
  15.9 0.3 reshape.178
  16.1 0.8 copy.26
  17.0 7.1 %all-to-all-done.2 = bf16[16,16,512]{2,1,0:T(8,128)(2,1)S(1)} async-done(((bf16[16,16,512]{2,1,0:T(8,128)(2,1)}), bf16[16,16,512]{2,1,0:T(8,128)(2,1)S(1)}, u32[]{:S(2)}, u32[]{:S(2)}) %all-to-all-start.2) | async-done | bytes 262176 | tf_op jit(solution)/shard_map/all_to_all | solution.py:108
  24.0 3.7 %all-to-all-start = ((bf16[16,24,512]{2,1,0:T(8,128)(2,1)}), bf16[16,24,512]{2,1,0:T(8,128)(2,1)S(1)}, u32[]{:S(2)}, u32[]{:S(2)}) async-start(bf16[16,24,512]{2,1,0:T(8,128)(2,1)} %bitcast.4), calls=%async_computation | async-start | bytes 786432 | tf_op jit(solution)/shard_map/all_to_all | solution.py:96
  27.8 1.8 %collective-permute-start.5 = (bf16[16,16,512]{2,1,0:T(8,128)(2,1)S(1)}, bf16[16,16,512]{2,1,0:T(8,128)(2,1)S(1)}, u32[]{:S(2)}, u32[]{:S(2)}) collective-permute-start(bf16[16,16,512]{2,1,0:T(8,128)(2,1)S(1)} %all-to-all-done.2), channel_id=1, source_target_pairs={{0,1},{1,0},{2,3},{3,2},{4,5},{5,4},{6,7},{7,6},{8,9},{9,8},{10,11... | collective-permute-start | bytes 786440 | tf_op jit(solution)/shard_map/ppermute | solution.py:16
  29.6 10.3 %all-to-all-done = bf16[16,24,512]{2,1,0:T(8,128)(2,1)S(1)} async-done(((bf16[16,24,512]{2,1,0:T(8,128)(2,1)}), bf16[16,24,512]{2,1,0:T(8,128)(2,1)S(1)}, u32[]{:S(2)}, u32[]{:S(2)}) %all-to-all-start) | async-done | bytes 393248 | tf_op jit(solution)/shard_map/all_to_all | solution.py:96
  39.8 0.6 collective-permute-start
  40.4 0.1 maximum_select_fusion.5
  40.5 0.9 collective-permute-start.6
  41.4 0.1 maximum_select_fusion.4
  41.5 6.2 %collective-permute-done = bf16[16,24,512]{2,1,0:T(8,128)(2,1)S(1)} collective-permute-done((bf16[16,24,512]{2,1,0:T(8,128)(2,1)S(1)}, bf16[16,24,512]{2,1,0:T(8,128)(2,1)S(1)}, u32[]{:S(2)}, u32[]{:S(2)}) %collective-permute-start) | collective-permute-done | bytes 393248 | tf_op jit(solution)/shard_map/ppermute | solution.py:16
  47.6 1.0 maximum_select_fusion.3
  48.7 1.5 collective-permute-start.1
  50.2 0.1 maximum_select_fusion.2
  50.3 5.0 %collective-permute-done.6 = bf16[16,16,2,512]{3,1,0,2:T(8,128)(2,1)S(1)} collective-permute-done((bf16[16,16,2,512]{3,1,0,2:T(8,128)(2,1)S(1)}, bf16[16,16,2,512]{3,1,0,2:T(8,128)(2,1)S(1)}, u32[]{:S(2)}, u32[]{:S(2)}) %collective-permute-start.6) | collective-permute-done | bytes 524320 | tf_op jit(solution)/shard_map/ppermute | solution.py:16
  55.3 0.2 maximum_select_fusion.1
  55.5 1.1 copy.32
  56.6 0.8 select_n.161
  57.4 6.8 %convolution_convert_fusion.1 = bf16[256,2048]{1,0:T(8,128)(2,1)} fusion(bf16[1024,2048]{1,0:T(8,128)(2,1)} %param.9, bf16[256,2048]{1,0:T(8,128)(2,1)S(1)} %select_n.161, bf16[2048,1024]{1,0:T(8,128)(2,1)} %param.8), kind=kOutput, calls=%fused_computation.4 | convolution fusion | flops 2148532224 | bytes 10485760 | tf_op jit(solution)/shard_map/dot_general | solution.py:25
  64.2 1.8 %reshape_reshape.9 = bf16[16,16,2,2,512]{4,3,2,1,0:T(2,128)(2,1)S(1)} reshape(bf16[256,2048]{1,0:T(8,128)(2,1)} %convolution_convert_fusion.1) | data formatting | bytes 2097152 | tf_op jit(solution)/shard_map/reshape;reshape | solution.py:81
  66.0 1.5 %constant_dynamic-slice_fusion = (bf16[16,16,1,2,512]{4,3,2,1,0:T(2,128)(2,1)S(1)}, bf16[16,16,1,2,512]{4,3,2,1,0:T(2,128)(2,1)}) fusion(bf16[16,16,2,2,512]{4,3,2,1,0:T(2,128)(2,1)S(1)} %reshape_reshape.9, s32[]{:T(128)S(6)} %select_n.150, s32[]{:T(128)S(6)} %select_n.149), kind=kLoop, calls=%fused_computation.49 | loop fusion | bytes 2097160 | tf_op jit(solution)/shard_map/jit(dynamic_index_in_dim)/dynamic_slice | solution.py:83
  67.6 0.9 copy.44
  68.4 3.9 %collective-permute-done.1 = bf16[16,24,2,512]{3,1,0,2:T(8,128)(2,1)} collective-permute-done((bf16[16,24,2,512]{3,1,0,2:T(8,128)(2,1)}, bf16[16,24,2,512]{3,1,0,2:T(8,128)(2,1)}, u32[]{:S(2)}, u32[]{:S(2)}) %collective-permute-start.1) | collective-permute-done | bytes 786464 | tf_op jit(solution)/shard_map/ppermute | solution.py:16
  72.3 1.6 %maximum_select_fusion = bf16[16,24,2,2,512]{4,1,0,3,2:T(8,128)(2,1)S(1)} fusion(bf16[16,24,1,2,512]{4,1,0,3,2:T(8,128)(2,1)} %bitcast.9, bf16[16,24,1,2,512]{4,1,0,3,2:T(8,128)(2,1)S(1)} %maximum_select_fusion.2, pred[]{:T(512)S(6)} %eq.26), kind=kLoop, calls=%fused_computation.9 | loop fusion | flops 2359296 | bytes 3145729 | tf_op jit(solution)/shard_map/jit(_where)/select_n | solution.py:75
  73.9 1.6 %copy.27 = bf16[16,24,2,2,512]{4,3,2,1,0:T(2,128)(2,1)S(1)} copy(bf16[16,24,2,2,512]{4,1,0,3,2:T(8,128)(2,1)S(1)} %maximum_select_fusion) | data formatting | bytes 3145728 | tf_op jit(solution)/shard_map/jit(_where)/select_n | solution.py:75
  75.5 2.4 %select_n.148 = bf16[384,2048]{1,0:T(8,128)(2,1)} reshape(bf16[16,24,2,2,512]{4,3,2,1,0:T(2,128)(2,1)S(1)} %copy.27) | data formatting | bytes 3145728 | tf_op jit(solution)/shard_map/jit(_where)/select_n | solution.py:75
  77.9 8.5 %convolution_convert_fusion = bf16[384,2048]{1,0:T(8,128)(2,1)} fusion(bf16[1024,2048]{1,0:T(8,128)(2,1)} %param.9, bf16[384,2048]{1,0:T(8,128)(2,1)} %select_n.148, bf16[2048,1024]{1,0:T(8,128)(2,1)} %param.8), kind=kOutput, calls=%fused_computation.3 | convolution fusion | flops 3222798336 | bytes 11534336 | tf_op jit(solution)/shard_map/dot_general | solution.py:25
  86.4 3.1 %reshape_reshape.8 = bf16[16,24,2,2,512]{4,3,2,1,0:T(2,128)(2,1)S(1)} reshape(bf16[384,2048]{1,0:T(8,128)(2,1)} %convolution_convert_fusion) | data formatting | bytes 3145728 | tf_op jit(solution)/shard_map/reshape;reshape | solution.py:81
  89.5 1.1 constant_dynamic-slice_fusion.2
  90.6 1.0 copy.42
  91.6 0.2 copy-done
  91.9 0.8 fusion.5
  92.7 1.9 %collective-permute-start.8 = (bf16[2,16,16,512]{3,2,1,0:T(8,128)(2,1)}, bf16[2,16,16,512]{3,2,1,0:T(8,128)(2,1)}, u32[]{:S(2)}, u32[]{:S(2)}) collective-permute-start(bf16[2,16,16,512]{3,2,1,0:T(8,128)(2,1)} %fusion.5), channel_id=1, source_target_pairs={{0,1},{1,0},{2,3},{3,2},{4,5},{5,4},{6,7},{7,6},{8,9},{9,8},{10,11... | collective-permute-start | bytes 1572872 | tf_op jit(solution)/shard_map/ppermute | solution.py:16
  94.6 0.1 copy.43
  94.7 9.7 %collective-permute-done.2 = bf16[16,24,2,512]{3,1,0,2:T(8,128)(2,1)S(1)} collective-permute-done((bf16[16,24,2,512]{3,1,0,2:T(8,128)(2,1)}, bf16[16,24,2,512]{3,1,0,2:T(8,128)(2,1)S(1)}, u32[]{:S(2)}, u32[]{:S(2)}) %collective-permute-start.2) | collective-permute-done | bytes 786464 | tf_op jit(solution)/shard_map/ppermute | solution.py:16
  104.4 1.0 fusion.2
  105.3 1.6 %collective-permute-start.3 = (bf16[2,16,24,512]{3,2,1,0:T(8,128)(2,1)}, bf16[2,16,24,512]{3,2,1,0:T(8,128)(2,1)}, u32[]{:S(2)}, u32[]{:S(2)}) collective-permute-start(bf16[2,16,24,512]{3,2,1,0:T(8,128)(2,1)} %fusion.2), channel_id=1, source_target_pairs={{0,1},{1,0},{2,3},{3,2},{4,5},{5,4},{6,7},{7,6},{8,9},{9,8},{10,11... | collective-permute-start | bytes 2359304 | tf_op jit(solution)/shard_map/ppermute | solution.py:16
  106.9 0.1 convert_reduce_fusion.3
  107.0 1.2 convert_reduce_fusion.2
  108.2 0.8 add_convert_fusion
  109.0 7.0 %all-to-all-start.3 = ((bf16[16,16,512]{2,1,0:T(8,128)(2,1)}), bf16[16,16,512]{2,1,0:T(8,128)(2,1)S(1)}, u32[]{:S(2)}, u32[]{:S(2)}) async-start(bf16[16,16,512]{2,1,0:T(8,128)(2,1)} %add_convert_fusion), calls=%async_computation.3 | async-start | bytes 524288 | tf_op jit(solution)/shard_map/all_to_all | solution.py:113
  116.0 0.1 convert_reduce_fusion.1
  116.1 4.4 %collective-permute-done.3 = bf16[2,16,24,512]{3,2,1,0:T(8,128)(2,1)} collective-permute-done((bf16[2,16,24,512]{3,2,1,0:T(8,128)(2,1)}, bf16[2,16,24,512]{3,2,1,0:T(8,128)(2,1)}, u32[]{:S(2)}, u32[]{:S(2)}) %collective-permute-start.3) | collective-permute-done | bytes 786464 | tf_op jit(solution)/shard_map/ppermute | solution.py:16
  120.5 1.3 convert_reduce_fusion
  121.8 1.0 add.95
  122.9 1.6 %all-to-all-done.3 = bf16[16,16,512]{2,1,0:T(8,128)(2,1)S(1)} async-done(((bf16[16,16,512]{2,1,0:T(8,128)(2,1)}), bf16[16,16,512]{2,1,0:T(8,128)(2,1)S(1)}, u32[]{:S(2)}, u32[]{:S(2)}) %all-to-all-start.3) | async-done | bytes 262176 | tf_op jit(solution)/shard_map/all_to_all | solution.py:113
  124.5 8.4 %all-to-all-start.1 = ((f32[16,24,512]{2,1,0:T(8,128)}), f32[16,24,512]{2,1,0:T(8,128)S(1)}, u32[]{:S(2)}, u32[]{:S(2)}) async-start(f32[16,24,512]{2,1,0:T(8,128)} %add.95), calls=%async_computation.1 | async-start | bytes 1572864 | tf_op jit(solution)/shard_map/all_to_all | solution.py:104
  133.0 1.5 %collective-permute-done.9 = bf16[16,16,512]{2,1,0:T(8,128)(2,1)S(1)} collective-permute-done((bf16[16,16,512]{2,1,0:T(8,128)(2,1)S(1)}, bf16[16,16,512]{2,1,0:T(8,128)(2,1)S(1)}, u32[]{:S(2)}, u32[]{:S(2)}) %collective-permute-start.9) | collective-permute-done | bytes 262176 | tf_op jit(solution)/shard_map/ppermute | solution.py:16
  134.6 0.3 copy.35
  134.9 0.2 copy.37
  135.1 11.9 %all-to-all-done.1 = f32[16,24,512]{2,1,0:T(8,128)S(1)} async-done(((f32[16,24,512]{2,1,0:T(8,128)}), f32[16,24,512]{2,1,0:T(8,128)S(1)}, u32[]{:S(2)}, u32[]{:S(2)}) %all-to-all-start.1) | async-done | bytes 786464 | tf_op jit(solution)/shard_map/all_to_all | solution.py:104
  146.9 0.5 copy.30
  147.4 0.2 copy.36
  147.7 0.1 pad_maximum_fusion
  147.8 1.0 gather_fusion
  148.8 0.9 multiply_convert_fusion
  (15 shorter events, 0.3 us)
Async XLA Ops:
  3.8 1.9 %collective-permute-start.4 = (bf16[16,16,512]{2,1,0:T(8,128)(2,1)S(1)}, bf16[16,16,512]{2,1,0:T(8,128)(2,1)}, u32[]{:S(2)}, u32[]{:S(2)}) collective-permute-start(bf16[16,16,512]{2,1,0:T(8,128)(2,1)S(1)} %bitcast.98), channel_id=1, source_target_pairs={{0,16},{16,0},{1,17},{17,1},{2,18},{18,2},{3,19},{19,3},{4,20},{20... | collective-permute-start | bytes 786440 | tf_op jit(solution)/shard_map/ppermute | solution.py:16
  5.6 18.4 %all-to-all-start.2 = ((bf16[16,16,512]{2,1,0:T(8,128)(2,1)}), bf16[16,16,512]{2,1,0:T(8,128)(2,1)S(1)}, u32[]{:S(2)}, u32[]{:S(2)}) async-start(bf16[16,16,512]{2,1,0:T(8,128)(2,1)} %collective-permute-done.4), calls=%async_computation.2 | async-start | bytes 524288 | tf_op jit(solution)/shard_map/all_to_all | solution.py:108
  24.0 15.8 %all-to-all-start = ((bf16[16,24,512]{2,1,0:T(8,128)(2,1)}), bf16[16,24,512]{2,1,0:T(8,128)(2,1)S(1)}, u32[]{:S(2)}, u32[]{:S(2)}) async-start(bf16[16,24,512]{2,1,0:T(8,128)(2,1)} %bitcast.4), calls=%async_computation | async-start | bytes 786432 | tf_op jit(solution)/shard_map/all_to_all | solution.py:96
  27.8 12.6 %collective-permute-start.5 = (bf16[16,16,512]{2,1,0:T(8,128)(2,1)S(1)}, bf16[16,16,512]{2,1,0:T(8,128)(2,1)S(1)}, u32[]{:S(2)}, u32[]{:S(2)}) collective-permute-start(bf16[16,16,512]{2,1,0:T(8,128)(2,1)S(1)} %all-to-all-done.2), channel_id=1, source_target_pairs={{0,1},{1,0},{2,3},{3,2},{4,5},{5,4},{6,7},{7,6},{8,9},{9,8},{10,11... | collective-permute-start | bytes 786440 | tf_op jit(solution)/shard_map/ppermute | solution.py:16
  39.8 7.8 %collective-permute-start = (bf16[16,24,512]{2,1,0:T(8,128)(2,1)S(1)}, bf16[16,24,512]{2,1,0:T(8,128)(2,1)S(1)}, u32[]{:S(2)}, u32[]{:S(2)}) collective-permute-start(bf16[16,24,512]{2,1,0:T(8,128)(2,1)S(1)} %all-to-all-done), channel_id=1, source_target_pairs={{0,1},{1,0},{2,3},{3,2},{4,5},{5,4},{6,7},{7,6},{8,9},{9,8},{10,11... | collective-permute-start | bytes 1179656 | tf_op jit(solution)/shard_map/ppermute | solution.py:16
  40.5 14.9 %collective-permute-start.6 = (bf16[16,16,2,512]{3,1,0,2:T(8,128)(2,1)S(1)}, bf16[16,16,2,512]{3,1,0,2:T(8,128)(2,1)S(1)}, u32[]{:S(2)}, u32[]{:S(2)}) collective-permute-start(bf16[16,16,2,512]{3,1,0,2:T(8,128)(2,1)S(1)} %maximum_select_fusion.5), channel_id=1, source_target_pairs={{0,2},{2,0},{1,3},{3,1},{4,6},{6,4},{5,7},{7,5},{8,10},{10,8},{9,1... | collective-permute-start | bytes 1572872 | tf_op jit(solution)/shard_map/ppermute | solution.py:16
  48.7 23.6 %collective-permute-start.1 = (bf16[16,24,2,512]{3,1,0,2:T(8,128)(2,1)}, bf16[16,24,2,512]{3,1,0,2:T(8,128)(2,1)}, u32[]{:S(2)}, u32[]{:S(2)}) collective-permute-start(bf16[16,24,2,512]{3,1,0,2:T(8,128)(2,1)} %maximum_select_fusion.3), channel_id=1, source_target_pairs={{0,2},{2,0},{1,3},{3,1},{4,6},{6,4},{5,7},{7,5},{8,10},{10,8},{9,1... | collective-permute-start | bytes 2359304 | tf_op jit(solution)/shard_map/ppermute | solution.py:16
  68.4 23.4 %collective-permute-start.7 = (bf16[16,16,2,512]{3,1,0,2:T(8,128)(2,1)}, bf16[16,16,2,512]{3,1,0,2:T(8,128)(2,1)S(1)}, u32[]{:S(2)}, u32[]{:S(2)}) collective-permute-start(bf16[16,16,2,512]{3,1,0,2:T(8,128)(2,1)} %bitcast.71), channel_id=1, source_target_pairs={{0,2},{2,0},{1,3},{3,1},{4,6},{6,4},{5,7},{7,5},{8,10},{10,8},{9,1... | collective-permute-start | bytes 1572872 | tf_op jit(solution)/shard_map/ppermute | solution.py:16
  90.6 1.2 copy-start
  91.6 12.8 %collective-permute-start.2 = (bf16[16,24,2,512]{3,1,0,2:T(8,128)(2,1)}, bf16[16,24,2,512]{3,1,0,2:T(8,128)(2,1)S(1)}, u32[]{:S(2)}, u32[]{:S(2)}) collective-permute-start(bf16[16,24,2,512]{3,1,0,2:T(8,128)(2,1)} %bitcast.69), channel_id=1, source_target_pairs={{0,2},{2,0},{1,3},{3,1},{4,6},{6,4},{5,7},{7,5},{8,10},{10,8},{9,1... | collective-permute-start | bytes 2359304 | tf_op jit(solution)/shard_map/ppermute | solution.py:16
  92.7 14.3 %collective-permute-start.8 = (bf16[2,16,16,512]{3,2,1,0:T(8,128)(2,1)}, bf16[2,16,16,512]{3,2,1,0:T(8,128)(2,1)}, u32[]{:S(2)}, u32[]{:S(2)}) collective-permute-start(bf16[2,16,16,512]{3,2,1,0:T(8,128)(2,1)} %fusion.5), channel_id=1, source_target_pairs={{0,1},{1,0},{2,3},{3,2},{4,5},{5,4},{6,7},{7,6},{8,9},{9,8},{10,11... | collective-permute-start | bytes 1572872 | tf_op jit(solution)/shard_map/ppermute | solution.py:16
  105.3 15.1 %collective-permute-start.3 = (bf16[2,16,24,512]{3,2,1,0:T(8,128)(2,1)}, bf16[2,16,24,512]{3,2,1,0:T(8,128)(2,1)}, u32[]{:S(2)}, u32[]{:S(2)}) collective-permute-start(bf16[2,16,24,512]{3,2,1,0:T(8,128)(2,1)} %fusion.2), channel_id=1, source_target_pairs={{0,1},{1,0},{2,3},{3,2},{4,5},{5,4},{6,7},{7,6},{8,9},{9,8},{10,11... | collective-permute-start | bytes 2359304 | tf_op jit(solution)/shard_map/ppermute | solution.py:16
  109.0 15.5 %all-to-all-start.3 = ((bf16[16,16,512]{2,1,0:T(8,128)(2,1)}), bf16[16,16,512]{2,1,0:T(8,128)(2,1)S(1)}, u32[]{:S(2)}, u32[]{:S(2)}) async-start(bf16[16,16,512]{2,1,0:T(8,128)(2,1)} %add_convert_fusion), calls=%async_computation.3 | async-start | bytes 524288 | tf_op jit(solution)/shard_map/all_to_all | solution.py:113
  124.5 22.5 %all-to-all-start.1 = ((f32[16,24,512]{2,1,0:T(8,128)}), f32[16,24,512]{2,1,0:T(8,128)S(1)}, u32[]{:S(2)}, u32[]{:S(2)}) async-start(f32[16,24,512]{2,1,0:T(8,128)} %add.95), calls=%async_computation.1 | async-start | bytes 1572864 | tf_op jit(solution)/shard_map/all_to_all | solution.py:104
  132.9 1.6 %collective-permute-start.9 = (bf16[16,16,512]{2,1,0:T(8,128)(2,1)S(1)}, bf16[16,16,512]{2,1,0:T(8,128)(2,1)S(1)}, u32[]{:S(2)}, u32[]{:S(2)}) collective-permute-start(bf16[16,16,512]{2,1,0:T(8,128)(2,1)S(1)} %all-to-all-done.3), channel_id=1, source_target_pairs={{0,16},{16,0},{1,17},{17,1},{2,18},{18,2},{3,19},{19,3},{4,20},{20... | collective-permute-start | bytes 786440 | tf_op jit(solution)/shard_map/ppermute | solution.py:16
  147.8 1.0 copy-start.1
where the time goes:
time: 151 us; the launch traced here: 150 us
  waiting for transfers between devices  62.7 us (42%)
  starting transfers between devices  36.2 us (24%)
  local copies, waits for them, and re-layouts  23.1 us (15%)
  matrix products  15.3 us (10%)
  other arithmetic  12.1 us (8%)
    ppermute x10, waiting for transfers between devices, from_partner(): return lax.ppermute(block, axis, route)  31.9 us
    dot_general x2, matrix products, feed(): jnp.dot(hidden, weight_out, preferred_element_type=jnp.float32)  15.3 us
    all_to_all x1, waiting for transfers between devices, body(): lax.all_to_all(summed, 'ep', split_axis=0, concat_axis=0, tiled=True)  11.9 us
    all_to_all x1, waiting for transfers between devices, body(): lax.all_to_all(narrow(main_buffer, capacity), 'ep', split_axis=0, concat_...  10.3 us
    ppermute x10, starting transfers between devices, from_partner(): return lax.ppermute(block, axis, route)  8.86 us
    all_to_all x1, starting transfers between devices, body(): lax.all_to_all(summed, 'ep', split_axis=0, concat_axis=0, tiled=True)  8.43 us
    all_to_all x1, starting transfers between devices, body(): lax.all_to_all(moved_rows, 'ep', split_axis=0, concat_axis=0, tiled=True)  8.22 us
    all_to_all x1, waiting for transfers between devices, body(): lax.all_to_all(moved_rows, 'ep', split_axis=0, concat_axis=0, tiled=True)  7.06 us
  transfers between devices with their start and end apart: 14, of which 11 were waited for; matrix products, arithmetic and copies ran while one was open for 29% of the time, Pallas kernels for 0%

commit v1 on v0

v1 whole, which is shorter than its diff:
```python
import functools

import jax
import jax.numpy as jnp
from jax import lax
from jax.experimental import pallas as pl
from jax.experimental.pallas import tpu as pltpu
from jax.sharding import PartitionSpec as P

SLICES = 4
CHUNKS = 4
BF16 = jnp.bfloat16
F32 = jnp.float32
MESH = pl.DeviceIdType.MESH


def layout(owner_count, tok_rows):
    groups = owner_count // SLICES
    chunks = min(CHUNKS, groups)
    per = groups // chunks
    seats = 3 * tok_rows // (4 * groups) + tok_rows // (2 * groups)
    unit = 8 if per == 1 else 16
    seats = -(-seats // unit) * unit
    offsets = [0]
    for far in range(1, groups // 2 + 1):
        offsets += [far, groups - far]
    return groups, chunks, per, seats, offsets[:groups]


def stack_rows(blocks):
    return jnp.concatenate([block.astype(F32) for block in blocks], axis=0).astype(BF16)


def kernel(
    owner_count,
    ids_col,
    ids_row,
    gates,
    tokens,
    weight_in,
    weight_out,
    out,
    w_in,
    w_out,
    send,
    gathered,
    staged,
    hidden,
    parts,
    diag_a,
    diag_b,
    from_x,
    from_y,
    sums,
    returned,
    w_sem,
    local_sem,
    z_send,
    z_recv,
    g_send,
    g_recv,
    r_send,
    r_recv,
    b_send,
    b_recv,
):
    tok_rows, width = tokens.shape
    groups, chunks, per, seats, offsets = layout(owner_count, tok_rows)
    half = width // 2
    me = lax.axis_index("ep")
    group = me // SLICES
    lane = me % SLICES
    x_bit, y_bit = lane % 2, lane // 2
    x_lane = y_bit * 2 + (1 - x_bit)
    y_lane = (1 - y_bit) * 2 + x_bit
    d_lane = (1 - y_bit) * 2 + (1 - x_bit)
    x_dev = group * SLICES + x_lane
    y_dev = group * SLICES + y_lane

    load_in = pltpu.make_async_copy(weight_in, w_in, w_sem.at[0])
    load_out = pltpu.make_async_copy(weight_out, w_out, w_sem.at[1])
    load_in.start()
    load_out.start()

    barrier = pltpu.get_barrier_semaphore()
    pl.semaphore_signal(barrier, inc=1, device_id={"ep": x_dev}, device_id_type=MESH)
    pl.semaphore_signal(barrier, inc=1, device_id={"ep": y_dev}, device_id_type=MESH)
    for off in range(1, groups):
        other = (group + off) % groups * SLICES + lane
        pl.semaphore_signal(barrier, inc=1, device_id={"ep": other}, device_id_type=MESH)

    slots = groups * seats
    lanes_e = -(-groups // 16) * 16
    t0 = lax.broadcasted_iota(jnp.int32, (tok_rows, tok_rows), 0)
    t1 = lax.broadcasted_iota(jnp.int32, (tok_rows, tok_rows), 1)
    ids_r = ids_row[...]
    hot_r = (lax.broadcasted_iota(jnp.int32, (lanes_e, tok_rows), 0) == ids_r).astype(F32)
    cum_r = jnp.dot(hot_r.astype(BF16), (t0 < t1).astype(F32).astype(BF16), preferred_element_type=F32)
    rank_r = jnp.sum(hot_r * cum_r, axis=0, keepdims=True).astype(jnp.int32)
    slot_r = ids_r * seats + rank_r
    place = (
        (lax.broadcasted_iota(jnp.int32, (slots, tok_rows), 0) == slot_r).astype(F32).astype(BF16)
    )
    step = 512
    for c in range(0, width, step):
        rows = jnp.dot(place, tokens[:, c : c + step], preferred_element_type=F32)
        for g in range(groups):
            send[g, :, c : c + step] = rows[g * seats : (g + 1) * seats].astype(BF16)

    pl.semaphore_wait(barrier, 2 + groups - 1)

    def remote(src, dst, s_sem, r_sem, dev):
        return pltpu.make_async_remote_copy(
            src_ref=src,
            dst_ref=dst,
            send_sem=s_sem,
            recv_sem=r_sem,
            device_id={"ep": dev},
            device_id_type=MESH,
        )

    def seat_block(ref, k):
        return ref.at[pl.ds(k % per * seats, seats)] if per > 1 else ref

    z_copies, local = {}, None
    for k in range(groups):
        target = (group - offsets[k] + groups) % groups
        dst = seat_block(gathered.at[k // per, lane], k)
        if k == 0:
            local = pltpu.make_async_copy(send.at[target], dst, local_sem.at[0])
            local.start()
        else:
            z_copies[k] = remote(
                send.at[target], dst, z_send.at[k], z_recv.at[k], target * SLICES + lane
            )
            z_copies[k].start()

    pending = list(z_copies.values())
    spread, forward, diag, pair, back = {}, {}, {}, {}, {}

    def stage_a(j):
        for k in range(j * per, (j + 1) * per):
            if k == 0:
                local.wait()
            else:
                z_copies[k].wait_recv()
        own = gathered.at[j, lane]
        spread[j] = [
            remote(own, own, g_send.at[j, 0], g_recv.at[j, 0], x_dev),
            remote(own, own, g_send.at[j, 1], g_recv.at[j, 1], y_dev),
        ]
        for copy in spread[j]:
            copy.start()

    def stage_b(j):
        first = gathered.at[j, x_lane, :, pl.ds(0, half)]
        second = gathered.at[j, y_lane, :, pl.ds(half, half)]
        forward[j] = [
            remote(first, first, g_send.at[j, 2], g_recv.at[j, 2], y_dev),
            remote(second, second, g_send.at[j, 3], g_recv.at[j, 3], x_dev),
        ]
        for arrived, onward in zip(spread[j], forward[j]):
            arrived.wait_recv()
            onward.start()

    def stage_c(j):
        for copy in forward[j]:
            copy.wait_recv()
        staged[...] = stack_rows([gathered[j, s] for s in range(SLICES)])
        if j == 0:
            load_in.wait()
        tile = 256
        rows = staged.shape[0] // SLICES

        @pl.loop(0, w_in.shape[1] // tile)
        def _(n):
            cols = pl.ds(pl.multiple_of(n * tile, tile), tile)
            value = jnp.dot(staged[...], w_in[:, cols], preferred_element_type=F32)
            hidden[:, cols] = jnp.maximum(value, 0.0).astype(BF16)

        if j == 0:
            load_out.wait()

        @pl.loop(0, width // tile)
        def _(n):
            cols = pl.ds(pl.multiple_of(n * tile, tile), tile)
            value = jnp.dot(hidden[...], w_out[:, cols], preferred_element_type=F32)
            for s in range(SLICES):
                parts[j, s, :, cols] = value[s * rows : (s + 1) * rows].astype(BF16)

    def stage_d(j):
        diag[j] = [
            remote(
                parts.at[j, d_lane, :, pl.ds(0, half)],
                diag_a.at[j],
                r_send.at[j, 0],
                r_recv.at[j, 0],
                y_dev,
            ),
            remote(
                parts.at[j, d_lane, :, pl.ds(half, half)],
                diag_b.at[j],
                r_send.at[j, 1],
                r_recv.at[j, 1],
                x_dev,
            ),
        ]
        for copy in diag[j]:
            copy.start()

    def stage_e(j):
        pair[j] = [
            remote(parts.at[j, x_lane], from_x.at[j], r_send.at[j, 2], r_recv.at[j, 2], x_dev),
            remote(parts.at[j, y_lane], from_y.at[j], r_send.at[j, 3], r_recv.at[j, 3], y_dev),
        ]
        diag[j][0].wait_recv()
        parts[j, x_lane, :, :half] = (
            parts[j, x_lane, :, :half].astype(F32) + diag_a[j].astype(F32)
        ).astype(BF16)
        diag[j][1].wait_recv()
        parts[j, y_lane, :, half:] = (
            parts[j, y_lane, :, half:].astype(F32) + diag_b[j].astype(F32)
        ).astype(BF16)
        for copy in pair[j]:
            copy.start()

    def stage_f(j):
        for copy in pair[j]:
            copy.wait_recv()
        sums[j] = (
            parts[j, lane].astype(F32) + from_x[j].astype(F32) + from_y[j].astype(F32)
        ).astype(BF16)
        for k in range(j * per, (j + 1) * per):
            source = (group + offsets[k]) % groups
            src = seat_block(sums.at[j], k)
            if k == 0:
                back[k] = pltpu.make_async_copy(src, returned.at[group], local_sem.at[1])
            else:
                back[k] = remote(
                    src, returned.at[group], b_send.at[k], b_recv.at[k], source * SLICES + lane
                )
            back[k].start()

    stages = [stage_a, stage_b, stage_c, stage_d, stage_e, stage_f]
    delay = [0, 1, 2, 2, 3, 4]
    for turn in range(chunks + max(delay)):
        for s in (0, 1, 4, 5, 2, 3):
            j = turn - delay[s]
            if 0 <= j < chunks:
                stages[s](j)

    ids_c = ids_col[...]
    hot_c = (lax.broadcasted_iota(jnp.int32, (tok_rows, 128), 1) == ids_c).astype(F32)
    cum_c = jnp.dot((t1 < t0).astype(F32).astype(BF16), hot_c.astype(BF16), preferred_element_type=F32)
    rank_c = jnp.sum(hot_c * cum_c, axis=1, keepdims=True).astype(jnp.int32)
    slot_c = ids_c * seats + rank_c
    pick = (
        (lax.broadcasted_iota(jnp.int32, (tok_rows, slots), 1) == slot_c).astype(F32).astype(BF16)
    )
    weight = gates[...]
    for k in range(groups):
        if k == 0:
            back[k].wait()
        else:
            back[k].wait_recv()
    for c in range(0, width, step):
        block = stack_rows([returned[g, :, c : c + step] for g in range(groups)])
        picked = jnp.dot(pick, block, preferred_element_type=F32)
        out[:, c : c + step] = (weight * picked).astype(BF16)

    for j in range(chunks):
        for copy in spread[j] + forward[j] + diag[j] + pair[j]:
            copy.wait_send()
    for k in range(1, groups):
        z_copies[k].wait_send()
        back[k].wait_send()


def body(tokens, gates, expert_ids, weight_in, weight_out):
    owner_count = lax.axis_size("ep")
    tok_rows, width = tokens.shape
    groups, chunks, per, seats, _ = layout(owner_count, tok_rows)
    rows = per * seats
    half = width // 2
    vmem = pl.BlockSpec(memory_space=pltpu.VMEM)
    hbm = pl.BlockSpec(memory_space=pl.ANY)
    dma = pltpu.SemaphoreType.DMA
    return pl.pallas_call(
        functools.partial(kernel, owner_count),
        out_shape=jax.ShapeDtypeStruct((tok_rows, width), BF16),
        in_specs=[vmem] * 4 + [hbm] * 2,
        out_specs=vmem,
        scratch_shapes=[
            pltpu.VMEM(weight_in.shape, BF16),
            pltpu.VMEM(weight_out.shape, BF16),
            pltpu.VMEM((groups, seats, width), BF16),
            pltpu.VMEM((chunks, SLICES, rows, width), BF16),
            pltpu.VMEM((SLICES * rows, width), BF16),
            pltpu.VMEM((SLICES * rows, weight_in.shape[1]), BF16),
            pltpu.VMEM((chunks, SLICES, rows, width), BF16),
            pltpu.VMEM((chunks, rows, half), BF16),
            pltpu.VMEM((chunks, rows, half), BF16),
            pltpu.VMEM((chunks, rows, width), BF16),
            pltpu.VMEM((chunks, rows, width), BF16),
            pltpu.VMEM((chunks, rows, width), BF16),
            pltpu.VMEM((groups, seats, width), BF16),
            dma((2,)),
            dma((2,)),
            dma((groups,)),
            dma((groups,)),
            dma((chunks, 4)),
            dma((chunks, 4)),
            dma((chunks, 4)),
            dma((chunks, 4)),
            dma((groups,)),
            dma((groups,)),
        ],
        compiler_params=pltpu.CompilerParams(
            collective_id=0, has_side_effects=True, vmem_limit_bytes=60 * 1024 * 1024
        ),
    )(
        expert_ids,
        expert_ids.reshape(1, tok_rows),
        gates.reshape(tok_rows, 1),
        tokens,
        weight_in,
        weight_out,
    )


def solution(mesh):
    in_specs = (
        P(("rep", "ep"), None),
        P(("rep", "ep")),
        P(("rep", "ep"), None),
        P(None, "ep"),
        P("ep", None),
    )
    out_specs = P(("rep", "ep"), None)
    return jax.shard_map(body, mesh=mesh, in_specs=in_specs, out_specs=out_specs, check_vma=False)
```

time: 151 us -> 70.7 us (0.47)
  Pallas kernels: 0 us -> 65 us
  waiting for transfers between devices: 62.7 us -> 0 us
  starting transfers between devices: 36.2 us -> 0 us
  local copies, waits for them, and re-layouts: 23.1 us -> 4.65 us
  matrix products: 15.3 us -> 0 us
  other arithmetic: 12.1 us -> 0 us
    pallas_call x0 -> x1, Pallas kernels: none -> 65 us  [body(): pl.pallas_call(functools.partial(kernel, owner_count), out_shape=jax.Shap...]
    ppermute x10 -> x0, waiting for transfers between devices: 31.9 us -> none  [from_partner(): return lax.ppermute(block, axis, route)]
    all_to_all x4 -> x0, waiting for transfers between devices: 30.8 us -> none  [the longest x1 11.9 us: body(): lax.all_to_all(summed, 'ep', split_axis=0, concat_axis=0, tiled=True)]
    all_to_all x4 -> x0, starting transfers between devices: 27.4 us -> none  [the longest x1 8.43 us: body(): lax.all_to_all(summed, 'ep', split_axis=0, concat_axis=0, tiled=True)]
    dot_general x2 -> x0, matrix products: 15.3 us -> none  [feed(): jnp.dot(hidden, weight_out, preferred_element_type=jnp.float32)]
    ppermute x10 -> x0, starting transfers between devices: 8.86 us -> none  [from_partner(): return lax.ppermute(block, axis, route)]
    select_n x4 -> x0, local copies, waits for them, and re-layouts: 5.94 us -> none  [gather_group(): jnp.where(high_bit == 0, jnp.stack([pair, across], -3), jnp.stack([across...]
    another operation x2 -> x0, local copies, waits for them, and re-layouts: 4.91 us -> none  [reduce_group(): split = part.reshape(part.shape[:-1] + (2, 2, quarter))]
  transfers between devices with their start and end apart: 14 -> 0, of which waited for: 11 -> 0; matrix products, arithmetic and copies ran while one was open for 29% -> 0% of each run, Pallas kernels for 0% -> 0%
where the time goes in v1:
time: 70.7 us; the launch traced here: 69.7 us
  Pallas kernels  65 us (92%)
  local copies, waits for them, and re-layouts  4.65 us (7%)
    pallas_call x1, Pallas kernels, body(): pl.pallas_call(functools.partial(kernel, owner_count), out_shape=jax.Shap...  65 us
    unnamed x2, local copies, waits for them, and re-layouts  3.27 us

profile of v1, /device:TPU:0, one launch (start us, length us, event | category | flops | bytes accessed | tf_op | source)
XLA Modules:
  0.0 69.7 jit_solution(4430405231260129651)
XLA Ops:
  0.0 1.4 %copy.7.gates = f32[128,1]{1,0:T(8,128)} copy(f32[128,1]{0,1:T(1,128)} %bitcast.3) | data formatting | bytes 1024 | tf_op jit(solution)/shard_map/reshape | solution.py:324
  1.4 1.4 %copy.6.ids_col = s32[128,1]{1,0:T(8,128)} copy(s32[128,1]{0,1:T(1,128)} %param.7) | data formatting | bytes 1024 | tf_op args[2]
  2.8 65.0 %shard_map.55 = bf16[128,2048]{1,0:T(8,128)(2,1)} custom-call(s32[128,1]{1,0:T(8,128)} %copy.6.ids_col, s32[1,128]{1,0:T(1,128)} %bitcast.2, f32[128,1]{1,0:T(8,128)} %copy.7.gates, bf16[128,2048]{1,0:T(8,128)(2,1)} %tokens.1, bf16[2048,1024]{1,0:T(8,128)(2,1)} %weight_in.1, bf16[1024,2048]{1,0:T(8,128)(2,1)} %weight_out.1), custom_call_target="tpu_custom_call" | custom-call | tf_op jit(solution)/shard_map/pallas_call | solution.py:288
  67.8 1.9 %copy.9 = bf16[128,2048]{1,0:T(8,128)(2,1)} copy(bf16[128,2048]{1,0:T(8,128)(2,1)} %shard_map.55) | data formatting | bytes 1048576

commit v2 on v1

--- a/solution.py
+++ b/solution.py
@@ -9,6 +9,8 @@
 
 SLICES = 4
 CHUNKS = 4
+STEP = 512
+ORDER = "a1b0a2b1c0a3b2c1d1b3c2d2e1c3d3e2d0f1e3f2e0f3f0"
 BF16 = jnp.bfloat16
 F32 = jnp.float32
 MESH = pl.DeviceIdType.MESH
@@ -16,7 +18,7 @@
 
 def layout(owner_count, tok_rows):
     groups = owner_count // SLICES
-    chunks = min(CHUNKS, groups)
+    chunks = CHUNKS
     per = groups // chunks
     seats = 3 * tok_rows // (4 * groups) + tok_rows // (2 * groups)
     unit = 8 if per == 1 else 16
@@ -33,7 +35,6 @@
 
 def kernel(
     owner_count,
-    ids_col,
     ids_row,
     gates,
     tokens,
@@ -54,7 +55,6 @@
     sums,
     returned,
     w_sem,
-    local_sem,
     z_send,
     z_recv,
     g_send,
@@ -89,25 +89,20 @@
         other = (group + off) % groups * SLICES + lane
         pl.semaphore_signal(barrier, inc=1, device_id={"ep": other}, device_id_type=MESH)
 
-    slots = groups * seats
     lanes_e = -(-groups // 16) * 16
     t0 = lax.broadcasted_iota(jnp.int32, (tok_rows, tok_rows), 0)
     t1 = lax.broadcasted_iota(jnp.int32, (tok_rows, tok_rows), 1)
-    ids_r = ids_row[...]
-    hot_r = (lax.broadcasted_iota(jnp.int32, (lanes_e, tok_rows), 0) == ids_r).astype(F32)
-    cum_r = jnp.dot(hot_r.astype(BF16), (t0 < t1).astype(F32).astype(BF16), preferred_element_type=F32)
-    rank_r = jnp.sum(hot_r * cum_r, axis=0, keepdims=True).astype(jnp.int32)
-    slot_r = ids_r * seats + rank_r
-    place = (
-        (lax.broadcasted_iota(jnp.int32, (slots, tok_rows), 0) == slot_r).astype(F32).astype(BF16)
-    )
-    step = 512
-    for c in range(0, width, step):
-        rows = jnp.dot(place, tokens[:, c : c + step], preferred_element_type=F32)
-        for g in range(groups):
-            send[g, :, c : c + step] = rows[g * seats : (g + 1) * seats].astype(BF16)
-
-    pl.semaphore_wait(barrier, 2 + groups - 1)
+    ids = ids_row[...]
+    hot = (lax.broadcasted_iota(jnp.int32, (lanes_e, tok_rows), 0) == ids).astype(F32)
+    ahead = jnp.dot(hot.astype(BF16), (t0 < t1).astype(F32).astype(BF16), preferred_element_type=F32)
+    slot = ids * seats + jnp.sum(hot * ahead, axis=0, keepdims=True).astype(jnp.int32)
+
+    def take(target, dst):
+        seat = lax.broadcasted_iota(jnp.int32, (seats, tok_rows), 0) + target * seats
+        place = (seat == slot).astype(F32).astype(BF16)
+        for c in range(0, width, STEP):
+            rows = jnp.dot(place, tokens[:, c : c + STEP], preferred_element_type=F32)
+            dst[:, c : c + STEP] = rows.astype(BF16)
 
     def remote(src, dst, s_sem, r_sem, dev):
         return pltpu.make_async_remote_copy(
@@ -122,27 +117,22 @@
     def seat_block(ref, k):
         return ref.at[pl.ds(k % per * seats, seats)] if per > 1 else ref
 
-    z_copies, local = {}, None
-    for k in range(groups):
+    spread, forward, diag, pair, z_copies, back = {}, {}, {}, {}, {}, {}
+
+    def take_for(k):
         target = (group - offsets[k] + groups) % groups
-        dst = seat_block(gathered.at[k // per, lane], k)
-        if k == 0:
-            local = pltpu.make_async_copy(send.at[target], dst, local_sem.at[0])
-            local.start()
-        else:
-            z_copies[k] = remote(
-                send.at[target], dst, z_send.at[k], z_recv.at[k], target * SLICES + lane
-            )
-            z_copies[k].start()
-
-    pending = list(z_copies.values())
-    spread, forward, diag, pair, back = {}, {}, {}, {}, {}
+        take(target, send.at[k])
+        z_copies[k] = remote(
+            send.at[k],
+            seat_block(gathered.at[k // per, lane], k),
+            z_send.at[k],
+            z_recv.at[k],
+            target * SLICES + lane,
+        )
 
     def stage_a(j):
         for k in range(j * per, (j + 1) * per):
-            if k == 0:
-                local.wait()
-            else:
+            if k > 0:
                 z_copies[k].wait_recv()
         own = gathered.at[j, lane]
         spread[j] = [
@@ -169,7 +159,7 @@
         staged[...] = stack_rows([gathered[j, s] for s in range(SLICES)])
         if j == 0:
             load_in.wait()
-        tile = 256
+        tile = STEP
         rows = staged.shape[0] // SLICES
 
         @pl.loop(0, w_in.shape[1] // tile)
@@ -231,42 +221,45 @@
             parts[j, lane].astype(F32) + from_x[j].astype(F32) + from_y[j].astype(F32)
         ).astype(BF16)
         for k in range(j * per, (j + 1) * per):
-            source = (group + offsets[k]) % groups
-            src = seat_block(sums.at[j], k)
-            if k == 0:
-                back[k] = pltpu.make_async_copy(src, returned.at[group], local_sem.at[1])
-            else:
+            if k > 0:
+                source = (group + offsets[k]) % groups
+                src = seat_block(sums.at[j], k)
                 back[k] = remote(
-                    src, returned.at[group], b_send.at[k], b_recv.at[k], source * SLICES + lane
+                    src, returned.at[k], b_send.at[k], b_recv.at[k], source * SLICES + lane
                 )
-            back[k].start()
-
-    stages = [stage_a, stage_b, stage_c, stage_d, stage_e, stage_f]
-    delay = [0, 1, 2, 2, 3, 4]
-    for turn in range(chunks + max(delay)):
-        for s in (0, 1, 4, 5, 2, 3):
-            j = turn - delay[s]
-            if 0 <= j < chunks:
-                stages[s](j)
-
-    ids_c = ids_col[...]
-    hot_c = (lax.broadcasted_iota(jnp.int32, (tok_rows, 128), 1) == ids_c).astype(F32)
-    cum_c = jnp.dot((t1 < t0).astype(F32).astype(BF16), hot_c.astype(BF16), preferred_element_type=F32)
-    rank_c = jnp.sum(hot_c * cum_c, axis=1, keepdims=True).astype(jnp.int32)
-    slot_c = ids_c * seats + rank_c
-    pick = (
-        (lax.broadcasted_iota(jnp.int32, (tok_rows, slots), 1) == slot_c).astype(F32).astype(BF16)
-    )
-    weight = gates[...]
+                back[k].start()
+
+    take(group, seat_block(gathered.at[0, lane], 0))
+    take_for(1)
+    pl.semaphore_wait(barrier, 2 + groups - 1)
+    if per == 1:
+        stage_a(0)
+    for k in range(2, groups):
+        take_for(k)
+        z_copies[k - 1].start()
+    z_copies[groups - 1].start()
+    if per > 1:
+        stage_a(0)
+
+    stages = {"a": stage_a, "b": stage_b, "c": stage_c, "d": stage_d, "e": stage_e, "f": stage_f}
+    for name, j in zip(ORDER[::2], ORDER[1::2]):
+        stages[name](int(j))
+
+    slot_c = jnp.sum(jnp.where(t0 == t1, slot, 0), axis=1, keepdims=True)
+    weight = jnp.sum(jnp.where(t0 == t1, gates[...], 0.0), axis=1, keepdims=True)
+    picks = []
     for k in range(groups):
-        if k == 0:
-            back[k].wait()
-        else:
+        if k > 0:
             back[k].wait_recv()
-    for c in range(0, width, step):
-        block = stack_rows([returned[g, :, c : c + step] for g in range(groups)])
-        picked = jnp.dot(pick, block, preferred_element_type=F32)
-        out[:, c : c + step] = (weight * picked).astype(BF16)
+        target = (group - offsets[k] + groups) % groups
+        seat = lax.broadcasted_iota(jnp.int32, (tok_rows, seats), 1) + target * seats
+        picks.append((seat == slot_c).astype(F32))
+    pick = jnp.concatenate(picks, axis=1).astype(BF16)
+    for c in range(0, width, STEP):
+        blocks = [sums[0, :seats, c : c + STEP]]
+        blocks += [returned[k, :, c : c + STEP] for k in range(1, groups)]
+        picked = jnp.dot(pick, stack_rows(blocks), preferred_element_type=F32)
+        out[:, c : c + STEP] = (weight * picked).astype(BF16)
 
     for j in range(chunks):
         for copy in spread[j] + forward[j] + diag[j] + pair[j]:
@@ -288,7 +281,7 @@
     return pl.pallas_call(
         functools.partial(kernel, owner_count),
         out_shape=jax.ShapeDtypeStruct((tok_rows, width), BF16),
-        in_specs=[vmem] * 4 + [hbm] * 2,
+        in_specs=[vmem] * 3 + [hbm] * 2,
         out_specs=vmem,
         scratch_shapes=[
             pltpu.VMEM(weight_in.shape, BF16),
@@ -305,7 +298,6 @@
             pltpu.VMEM((chunks, rows, width), BF16),
             pltpu.VMEM((groups, seats, width), BF16),
             dma((2,)),
-            dma((2,)),
             dma((groups,)),
             dma((groups,)),
             dma((chunks, 4)),
@@ -319,9 +311,8 @@
             collective_id=0, has_side_effects=True, vmem_limit_bytes=60 * 1024 * 1024
         ),
     )(
-        expert_ids,
         expert_ids.reshape(1, tok_rows),
-        gates.reshape(tok_rows, 1),
+        gates.reshape(1, tok_rows),
         tokens,
         weight_in,
         weight_out,

time: 70.7 us -> 59.1 us (0.84); the launches traced: 69.7 us -> 58.9 us
  Pallas kernels: 65 us -> 57 us
  local copies, waits for them, and re-layouts: 4.65 us -> 1.88 us
    pallas_call x1, Pallas kernels: 65 us -> 57 us  [body(): pl.pallas_call(functools.partial(kernel, owner_count), out_shape=jax.Shap...]
    unnamed x2 -> x1, local copies, waits for them, and re-layouts: 3.27 us -> 1.88 us
    reshape x1 -> x0, local copies, waits for them, and re-layouts: 1.38 us -> none  [body(): gates.reshape(tok_rows, 1)]
where the time goes in v2:
time: 59.1 us; the launch traced here: 58.9 us
  Pallas kernels  57 us (96%)
  local copies, waits for them, and re-layouts  1.88 us (3%)
    pallas_call x1, Pallas kernels, body(): pl.pallas_call(functools.partial(kernel, owner_count), out_shape=jax.Shap...  57 us
    unnamed x1, local copies, waits for them, and re-layouts  1.88 us

profile of v2, /device:TPU:0, one launch (start us, length us, event | category | flops | bytes accessed | tf_op | source)
XLA Modules:
  0.0 58.9 jit_solution(6017493584363893829)
XLA Ops:
  0.0 57.0 %shard_map.55 = bf16[128,2048]{1,0:T(8,128)(2,1)} custom-call(s32[1,128]{1,0:T(1,128)} %bitcast.2, f32[1,128]{1,0:T(1,128)} %bitcast.3, bf16[128,2048]{1,0:T(8,128)(2,1)} %tokens.1, bf16[2048,1024]{1,0:T(8,128)(2,1)} %weight_in.1, bf16[1024,2048]{1,0:T(8,128)(2,1)} %weight_out.1), custom_call_target="tpu_custom_call" | custom-call | tf_op jit(solution)/shard_map/pallas_call | solution.py:281
  57.0 1.9 %copy.7 = bf16[128,2048]{1,0:T(8,128)(2,1)} copy(bf16[128,2048]{1,0:T(8,128)(2,1)} %shard_map.55) | data formatting | bytes 1048576

commit v3 on v2

--- a/solution.py
+++ b/solution.py
@@ -207,12 +207,12 @@
         parts[j, x_lane, :, :half] = (
             parts[j, x_lane, :, :half].astype(F32) + diag_a[j].astype(F32)
         ).astype(BF16)
+        pair[j][0].start()
         diag[j][1].wait_recv()
         parts[j, y_lane, :, half:] = (
             parts[j, y_lane, :, half:].astype(F32) + diag_b[j].astype(F32)
         ).astype(BF16)
-        for copy in pair[j]:
-            copy.start()
+        pair[j][1].start()
 
     def stage_f(j):
         for copy in pair[j]:

time: 59.1 us -> 59.1 us (level)
  no operation moved by 1% of the time
where the time goes in v3:
time: 59.1 us; the launch traced here: 58.9 us
  Pallas kernels  57 us (96%)
  local copies, waits for them, and re-layouts  1.88 us (3%)
    pallas_call x1, Pallas kernels, body(): pl.pallas_call(functools.partial(kernel, owner_count), out_shape=jax.Shap...  57 us
    unnamed x1, local copies, waits for them, and re-layouts  1.88 us

profile of v3, /device:TPU:0, one launch (start us, length us, event | category | flops | bytes accessed | tf_op | source)
XLA Modules:
  0.0 58.9 jit_solution(14032560193628394321)
XLA Ops:
  0.0 57.0 %shard_map.55 = bf16[128,2048]{1,0:T(8,128)(2,1)} custom-call(s32[1,128]{1,0:T(1,128)} %bitcast.2, f32[1,128]{1,0:T(1,128)} %bitcast.3, bf16[128,2048]{1,0:T(8,128)(2,1)} %tokens.1, bf16[2048,1024]{1,0:T(8,128)(2,1)} %weight_in.1, bf16[1024,2048]{1,0:T(8,128)(2,1)} %weight_out.1), custom_call_target="tpu_custom_call" | custom-call | tf_op jit(solution)/shard_map/pallas_call | solution.py:281
  57.0 1.9 %copy.7 = bf16[128,2048]{1,0:T(8,128)(2,1)} copy(bf16[128,2048]{1,0:T(8,128)(2,1)} %shard_map.55) | data formatting | bytes 1048576
